TPU v7x, 32 devices: a whole 2x2x4 slice. The times are simulated.
32 devices in a mesh: gx: 4 (over y, x), gy: 2 (over core), gz: 4 (over z).
Axes of the slice: x: 2, y: 2, z: 4, core: 2. Of those that a mesh axis runs over, the one named last changes fastest.
Arguments:
- phi_start: float32 [64, 96, 512], P('gx', 'gy', 'gz'), may hold values from -30 to 30
Outputs:
- phi_final: float32 [64, 96, 512], P('gx', 'gy', 'gz')
- residuals: float32 [3], replicated
All inputs are finite; a program needn't handle non-finite values.
Results may differ from a plain program's by a relative error of at most 0.0003.
Values sent between devices are 32-bit elements; how exact they have to be, the bound alone decides.
No kernel may reach another device: no remote copies, remote signals or barrier semaphores. Data moves between devices by JAX's collectives and lax.ppermute only.
A program may use at most 64 MiB of HBM per device.

v0:
```python
import jax
import jax.numpy as jnp
from jax import lax
from jax.sharding import PartitionSpec as P

ITERS = 3
pseudo_step = 0.45


def extended_2(cells, sides, width):
    for axis, dim in sides:
        count = lax.axis_size(axis)
        ends = count - 1
        head = lax.slice_in_dim(cells, 0, width, axis=dim)
        tail = lax.slice_in_dim(cells, cells.shape[dim] - width, cells.shape[dim], axis=dim)
        cells = jnp.concatenate(
            [
                lax.ppermute(tail, axis, [(i, (i + 1) % count) for i in range(ends)]),
                cells,
                lax.ppermute(head, axis, [((i + 1) % count, i) for i in range(ends)]),
            ],
            axis=dim,
        )
    return cells


def smooth_sign(field):
    return field / jnp.sqrt(field * field + 1.0)


def upwind_term(back, fwd, positive):
    plus = jnp.maximum(jnp.maximum(back, 0.0) ** 2, jnp.minimum(fwd, 0.0) ** 2)
    minus = jnp.maximum(jnp.minimum(back, 0.0) ** 2, jnp.maximum(fwd, 0.0) ** 2)
    return jnp.where(positive, plus, minus)


def update(ext, sgn):
    center = ext[1:-1, 1:-1, 1:-1]
    positive = sgn > 0.0
    total = upwind_term(center - ext[:-2, 1:-1, 1:-1], ext[2:, 1:-1, 1:-1] - center, positive)
    total = total + upwind_term(
        center - ext[1:-1, :-2, 1:-1], ext[1:-1, 2:, 1:-1] - center, positive
    )
    total = total + upwind_term(
        center - ext[1:-1, 1:-1, :-2], ext[1:-1, 1:-1, 2:] - center, positive
    )
    return center - pseudo_step * sgn * (jnp.sqrt(total) - 1.0)


def clamp_axis(field, margin, dim, count, place):
    length = field.shape[dim]
    position = lax.broadcasted_iota(jnp.int32, field.shape, dim)
    low_value = lax.slice_in_dim(field, margin, margin + 1, axis=dim)
    high_value = lax.slice_in_dim(field, length - margin - 1, length - margin, axis=dim)
    field = jnp.where((place == 0) & (position < margin), low_value, field)
    return jnp.where((place == count - 1) & (position >= length - margin), high_value, field)


def clamp_edges(field, margin):
    field = clamp_axis(field, margin, 0, lax.axis_size("gx"), lax.axis_index("gx"))
    field = clamp_axis(field, margin, 1, lax.axis_size("gy"), lax.axis_index("gy"))
    return clamp_axis(field, margin, 2, lax.axis_size("gz"), lax.axis_index("gz"))


def crop(field, margin):
    if margin == 0:
        return field
    return field[margin:-margin, margin:-margin, margin:-margin]


def reduce_now(partial_value):
    return lax.psum(partial_value, ("gx", "gy", "gz"))


def local(phi_start):
    partials = []
    extended = extended_2(phi_start, (("gx", 0), ("gy", 1), ("gz", 2)), ITERS)
    extended = clamp_edges(extended, ITERS)
    sign_wide = smooth_sign(extended)
    current = extended
    for step in range(ITERS):
        margin = ITERS - step
        newer = update(current, crop(sign_wide, step + 1))
        difference = crop(newer, margin - 1) - crop(current, margin)
        partials.append(reduce_now(jnp.sum(difference * difference)))
        if margin - 1 > 0:
            newer = clamp_edges(newer, margin - 1)
        current = newer
    stacked = jnp.stack(partials)
    cells = phi_start.shape[0] * phi_start.shape[1] * phi_start.shape[2]
    cells = cells * lax.axis_size("gx") * lax.axis_size("gy") * lax.axis_size("gz")
    residuals = jnp.sqrt(stacked / jnp.float32(cells)) / pseudo_step
    return (current, residuals)


def solution(mesh):
    return jax.shard_map(
        local,
        mesh=mesh,
        in_specs=(P("gx", "gy", "gz"),),
        out_specs=(P("gx", "gy", "gz"), P()),
        check_vma=False,
    )
```

profile of v0, /device:TPU:0, one launch (start us, length us, event | category | flops | bytes accessed | tf_op | source)
XLA Modules:
  0.0 102.0 jit_solution(16079190205514697008)
XLA Ops:
  0.6 1.1 %copy.19 = f32[16,48,128]{2,0,1:T(8,128)S(1)} copy(f32[16,48,128]{2,1,0:T(8,128)} %param.1) | data formatting | bytes 786432 | tf_op args[0]
  1.8 4.9 %collective-permute-start = (f32[3,48,128]{2,0,1:T(4,128)S(1)}, f32[3,48,128]{2,0,1:T(4,128)S(1)}, u32[]{:S(2)}, u32[]{:S(2)}) collective-permute-start(f32[3,48,128]{2,0,1:T(4,128)S(1)} %get-tuple-element.35), channel_id=1, source_target_pairs={{0,8},{8,16},{16,24},{1,9},{9,17},{17,25},{2,10},{10,18},{18,26},{... | collective-permute-start | bytes 221192 | tf_op jit(solution)/shard_map/ppermute | solution.py:18
  6.7 1.3 %collective-permute-start.1 = (f32[3,48,128]{2,0,1:T(4,128)S(1)}, f32[3,48,128]{2,0,1:T(4,128)S(1)}, u32[]{:S(2)}, u32[]{:S(2)}) collective-permute-start(f32[3,48,128]{2,0,1:T(4,128)S(1)} %get-tuple-element.36), channel_id=1, source_target_pairs={{8,0},{16,8},{24,16},{9,1},{17,9},{25,17},{10,2},{18,10},{26,18},{... | collective-permute-start | bytes 221192 | tf_op jit(solution)/shard_map/ppermute | solution.py:20
  8.1 0.6 compare_and_fusion.4
  8.7 0.5 compare_and_fusion.6
  9.2 0.5 compare_and_fusion.3
  9.7 0.6 compare_and_fusion.2
  10.3 0.0 collective-permute-done
  10.3 2.9 %collective-permute-done.1 = f32[3,48,128]{2,0,1:T(4,128)S(1)} collective-permute-done((f32[3,48,128]{2,0,1:T(4,128)S(1)}, f32[3,48,128]{2,0,1:T(4,128)S(1)}, u32[]{:S(2)}, u32[]{:S(2)}) %collective-permute-start.1) | collective-permute-done | bytes 73760 | tf_op jit(solution)/shard_map/ppermute | solution.py:20
  13.2 1.3 %collective-permute-start.2 = (f32[22,3,128]{2,0,1:T(8,128)S(1)}, f32[22,3,128]{2,0,1:T(8,128)S(1)}, u32[]{:S(2)}, u32[]{:S(2)}) collective-permute-start(f32[22,3,128]{2,0,1:T(8,128)S(1)} %get-tuple-element.33), channel_id=1, source_target_pairs={{0,4},{1,5},{2,6},{3,7},{8,12},{9,13},{10,14},{11,15},{16,20},{17,... | collective-permute-start | bytes 101384 | tf_op jit(solution)/shard_map/ppermute | solution.py:18
  14.5 1.3 %collective-permute-start.3 = (f32[22,3,128]{2,0,1:T(8,128)S(1)}, f32[22,3,128]{2,0,1:T(8,128)S(1)}, u32[]{:S(2)}, u32[]{:S(2)}) collective-permute-start(f32[22,3,128]{2,0,1:T(8,128)S(1)} %get-tuple-element.34), channel_id=1, source_target_pairs={{4,0},{5,1},{6,2},{7,3},{12,8},{13,9},{14,10},{15,11},{20,16},{21,... | collective-permute-start | bytes 101384 | tf_op jit(solution)/shard_map/ppermute | solution.py:20
  15.8 0.6 compare_and_fusion.1
  16.4 0.0 collective-permute-done.2
  16.4 1.2 %collective-permute-done.3 = f32[22,3,128]{2,0,1:T(8,128)S(1)} collective-permute-done((f32[22,3,128]{2,0,1:T(8,128)S(1)}, f32[22,3,128]{2,0,1:T(8,128)S(1)}, u32[]{:S(2)}, u32[]{:S(2)}) %collective-permute-start.3) | collective-permute-done | bytes 33824 | tf_op jit(solution)/shard_map/ppermute | solution.py:20
  17.6 0.1 pad_maximum_fusion.1
  17.7 0.2 fusion.12
  18.0 0.3 copy.22
  18.3 3.5 %collective-permute-start.4 = (f32[22,54,3]{1,0,2:T(8,128)S(1)}, f32[22,54,3]{1,0,2:T(8,128)S(1)}, u32[]{:S(2)}, u32[]{:S(2)}) collective-permute-start(f32[22,54,3]{1,0,2:T(8,128)S(1)} %copy.22), channel_id=1, source_target_pairs={{0,1},{1,2},{2,3},{4,5},{5,6},{6,7},{8,9},{9,10},{10,11},{12,13},{... | collective-permute-start | bytes 42776 | tf_op jit(solution)/shard_map/ppermute | solution.py:18
  21.8 0.3 copy.23
  22.1 1.3 %collective-permute-start.5 = (f32[22,54,3]{1,0,2:T(8,128)S(1)}, f32[22,54,3]{1,0,2:T(8,128)S(1)}, u32[]{:S(2)}, u32[]{:S(2)}) collective-permute-start(f32[22,54,3]{1,0,2:T(8,128)S(1)} %copy.23), channel_id=1, source_target_pairs={{1,0},{2,1},{3,2},{5,4},{6,5},{7,6},{9,8},{10,9},{11,10},{13,12},{... | collective-permute-start | bytes 42776 | tf_op jit(solution)/shard_map/ppermute | solution.py:20
  23.4 0.5 compare_and_fusion
  23.9 0.0 collective-permute-done.4
  23.9 0.4 copy.24
  24.3 3.7 %collective-permute-done.5 = f32[22,54,3]{1,0,2:T(8,128)S(1)} collective-permute-done((f32[22,54,3]{1,0,2:T(8,128)S(1)}, f32[22,54,3]{1,0,2:T(8,128)S(1)}, u32[]{:S(2)}, u32[]{:S(2)}) %collective-permute-start.5) | collective-permute-done | bytes 14288 | tf_op jit(solution)/shard_map/ppermute | solution.py:20
  27.9 0.4 copy.25
  28.3 0.8 pad_maximum_fusion
  29.1 0.1 fusion.7
  29.2 0.8 select_select_fusion.2
  30.1 0.0 copy-done.4
  30.1 0.0 copy-done.5
  30.1 1.0 %select_select_fusion.1 = f32[22,54,134]{2,0,1:T(8,128)S(1)} fusion(f32[22,134]{1,0:T(8,128)S(1)} %get-tuple-element.16, f32[22,134]{1,0:T(8,128)S(1)} %get-tuple-element.15, pred[54]{0:T(512)(128)(4,1)S(1)} %get-tuple-element.41, pred[54]{0:T(512)(128)(4,1)S(1)} %get-tuple-element.42, f32[54,134]{1,0:T(8,128)S(1)} %get-tuple-element.37, ...), kind=kLoop, calls=%fused_computation.3 | loop fusion | flops 1591920 | bytes 1355160 | tf_op jit(solution)/shard_map/jit(_where)/select_n | solution.py:56
  31.1 0.4 fusion.6
  31.6 0.4 copy.39
  32.0 0.4 copy.40
  32.4 3.3 %rsqrt_multiply_fusion = (f32[22,54,134]{2,0,1:T(8,128)S(1)}, f32[22,54,134]{2,0,1:T(8,128)S(1)}) fusion(f32[22,54]{0,1:T(8,128)S(1)} %bitcast.56, pred[134]{0:T(512)(128)(4,1)} %get-tuple-element.43, f32[22,54]{0,1:T(8,128)S(1)} %bitcast.55, pred[134]{0:T(512)(128)(4,1)} %get-tuple-element.44, f32[22,134]{1,0:T(8,128)S(1)} %get-tuple-element.16, ...), kind=kLoop, calls=%fused_computation.1 | loop fusion | flops 2387880 | bytes 2001700 | tf_op jit(solution)/shard_map/div | solution.py:28
  35.7 3.2 %multiply_subtract_fusion = f32[20,52,132]{2,0,1:T(8,128)S(1)} fusion(f32[22,54,134]{2,0,1:T(8,128)S(1)} %get-tuple-element.12, f32[22,54,134]{2,0,1:T(8,128)S(1)} %get-tuple-element.11), kind=kLoop, calls=%fused_computation.14 | loop fusion | flops 6314880 | bytes 4942080 | tf_op jit(solution)/shard_map/sub | solution.py:47
  38.9 1.0 %fusion.3 = f32[]{:T(128)} fusion(f32[22,54,134]{2,0,1:T(8,128)S(1)} %get-tuple-element.12, f32[20,52,132]{2,0,1:T(8,128)S(1)} %multiply_subtract_fusion), kind=kLoop, calls=%fused_computation.31 | loop fusion | flops 294911 | bytes 786436 | tf_op jit(solution)/shard_map/reduce_sum | solution.py:85
  40.0 0.1 fusion.9
  40.1 0.0 copy-start.2
  40.1 0.0 copy-start.3
  40.1 0.2 select_select_fusion.5
  40.4 0.4 copy-done.2
  40.8 0.5 select_select_fusion.4
  41.3 1.5 %fusion.8 = (f32[20,52,1]{2,0,1:T(8,128)}, f32[20,52,1]{2,0,1:T(8,128)}) fusion(f32[20,52,132]{2,0,1:T(8,128)S(1)} %select_select_fusion.4), kind=kLoop, calls=%fused_computation.78 | loop fusion | bytes 16640 | tf_op jit(solution)/shard_map/slice | solution.py:54
  42.8 1.5 %copy.42 = f32[20,52,1]{0,1,2:T(8,128)S(1)} copy(f32[20,52,1]{2,0,1:T(8,128)} %get-tuple-element.20) | data formatting | bytes 8320 | tf_op jit(solution)/shard_map/jit(_where)/broadcast_in_dim | solution.py:55
  44.3 1.5 %copy.41 = f32[20,52,1]{0,1,2:T(8,128)S(1)} copy(f32[20,52,1]{2,0,1:T(8,128)} %get-tuple-element.19) | data formatting | bytes 8320 | tf_op jit(solution)/shard_map/jit(_where)/broadcast_in_dim | solution.py:56
  45.8 0.0 copy-done.8
  45.8 0.6 select_select_fusion.3
  46.5 0.0 copy-start
  46.5 3.1 %multiply_subtract_fusion.1 = f32[18,50,130]{2,0,1:T(8,128)S(1)} fusion(f32[20,52,132]{2,0,1:T(8,128)S(1)} %select_select_fusion.3, f32[22,54,134]{2,0,1:T(8,128)S(1)} %get-tuple-element.11), kind=kLoop, calls=%fused_computation.24 | loop fusion | flops 5382000 | bytes 4212000 | tf_op jit(solution)/shard_map/sub | solution.py:47
  49.6 1.0 fusion.1
  50.6 0.1 fusion.11
  50.7 0.2 select_select_fusion.8
  51.0 0.4 copy-done.6
  51.4 0.0 copy-done.7
  51.4 0.5 select_select_fusion.7
  51.9 1.2 %fusion.10 = (f32[18,50,1]{2,0,1:T(8,128)}, f32[18,50,1]{2,0,1:T(8,128)}) fusion(f32[18,50,130]{2,0,1:T(8,128)S(1)} %select_select_fusion.7), kind=kLoop, calls=%fused_computation.80 | loop fusion | bytes 14400 | tf_op jit(solution)/shard_map/slice | solution.py:54
  53.2 1.5 %copy.43 = f32[18,50,1]{0,1,2:T(8,128)S(1)} copy(f32[18,50,1]{2,0,1:T(8,128)} %get-tuple-element.25) | data formatting | bytes 7200 | tf_op jit(solution)/shard_map/jit(_where)/broadcast_in_dim | solution.py:56
  54.7 1.5 %copy.44 = f32[18,50,1]{0,1,2:T(8,128)S(1)} copy(f32[18,50,1]{2,0,1:T(8,128)} %get-tuple-element.26) | data formatting | bytes 7200 | tf_op jit(solution)/shard_map/jit(_where)/broadcast_in_dim | solution.py:55
  56.2 0.6 select_select_fusion.6
  56.8 1.6 %multiply_reduce_fusion = (f32[]{:T(128)}, f32[16,48,128]{2,0,1:T(8,128)S(1)}) fusion(f32[18,50,130]{2,0,1:T(8,128)S(1)} %select_select_fusion.6, f32[22,54,134]{2,0,1:T(8,128)S(1)} %get-tuple-element.11), kind=kLoop, calls=%fused_computation.38 | loop fusion | flops 4816895 | bytes 3538948 | tf_op jit(solution)/shard_map/reduce_sum | solution.py:85
  58.4 0.9 copy.38
  59.3 40.2 %all-reduce = (f32[1]{0:T(128)}, f32[1]{0:T(128)}, f32[1]{0:T(128)}) all-reduce(f32[1]{0:T(128)} %bitcast.20, f32[1]{0:T(128)} %bitcast.19, f32[1]{0:T(128)} %bitcast.18), channel_id=1, replica_groups=mesh['gx'=4,'gy'=2,'gz'=4] {'gx','gy','gz'}, use_global_device_ids=true, to_apply=%region_5.6 | all-reduce | flops 3 | bytes 24 | tf_op jit(solution)/shard_map/psum | solution.py:72
  99.5 2.5 %fusion.5 = f32[3]{0:T(128)} fusion(f32[1]{0:T(128)} %get-tuple-element.6, f32[1]{0:T(128)} %get-tuple-element.7, f32[1]{0:T(128)} %get-tuple-element.8), kind=kLoop, calls=%fused_computation.75 | loop fusion | flops 12 | bytes 24 | tf_op jit(solution)/shard_map/div | solution.py:92
  (28 shorter events, 0.2 us)
Async XLA Ops:
  1.8 8.5 %collective-permute-start = (f32[3,48,128]{2,0,1:T(4,128)S(1)}, f32[3,48,128]{2,0,1:T(4,128)S(1)}, u32[]{:S(2)}, u32[]{:S(2)}) collective-permute-start(f32[3,48,128]{2,0,1:T(4,128)S(1)} %get-tuple-element.35), channel_id=1, source_target_pairs={{0,8},{8,16},{16,24},{1,9},{9,17},{17,25},{2,10},{10,18},{18,26},{... | collective-permute-start | bytes 221192 | tf_op jit(solution)/shard_map/ppermute | solution.py:18
  6.7 6.5 %collective-permute-start.1 = (f32[3,48,128]{2,0,1:T(4,128)S(1)}, f32[3,48,128]{2,0,1:T(4,128)S(1)}, u32[]{:S(2)}, u32[]{:S(2)}) collective-permute-start(f32[3,48,128]{2,0,1:T(4,128)S(1)} %get-tuple-element.36), channel_id=1, source_target_pairs={{8,0},{16,8},{24,16},{9,1},{17,9},{25,17},{10,2},{18,10},{26,18},{... | collective-permute-start | bytes 221192 | tf_op jit(solution)/shard_map/ppermute | solution.py:20
  8.0 22.0 %copy-start.4 = (pred[54]{0:T(512)(128)(4,1)}, pred[54]{0:T(512)(128)(4,1)S(1)}, u32[]{:S(2)}) copy-start(pred[54]{0:T(512)(128)(4,1)S(1)} %get-tuple-element.41) | copy-start | bytes 166
  8.1 22.0 %copy-start.5 = (pred[54]{0:T(512)(128)(4,1)}, pred[54]{0:T(512)(128)(4,1)S(1)}, u32[]{:S(2)}) copy-start(pred[54]{0:T(512)(128)(4,1)S(1)} %get-tuple-element.42) | copy-start | bytes 166
  13.2 3.2 %collective-permute-start.2 = (f32[22,3,128]{2,0,1:T(8,128)S(1)}, f32[22,3,128]{2,0,1:T(8,128)S(1)}, u32[]{:S(2)}, u32[]{:S(2)}) collective-permute-start(f32[22,3,128]{2,0,1:T(8,128)S(1)} %get-tuple-element.33), channel_id=1, source_target_pairs={{0,4},{1,5},{2,6},{3,7},{8,12},{9,13},{10,14},{11,15},{16,20},{17,... | collective-permute-start | bytes 101384 | tf_op jit(solution)/shard_map/ppermute | solution.py:18
  14.5 3.1 %collective-permute-start.3 = (f32[22,3,128]{2,0,1:T(8,128)S(1)}, f32[22,3,128]{2,0,1:T(8,128)S(1)}, u32[]{:S(2)}, u32[]{:S(2)}) collective-permute-start(f32[22,3,128]{2,0,1:T(8,128)S(1)} %get-tuple-element.34), channel_id=1, source_target_pairs={{4,0},{5,1},{6,2},{7,3},{12,8},{13,9},{14,10},{15,11},{20,16},{21,... | collective-permute-start | bytes 101384 | tf_op jit(solution)/shard_map/ppermute | solution.py:20
  18.3 5.6 %collective-permute-start.4 = (f32[22,54,3]{1,0,2:T(8,128)S(1)}, f32[22,54,3]{1,0,2:T(8,128)S(1)}, u32[]{:S(2)}, u32[]{:S(2)}) collective-permute-start(f32[22,54,3]{1,0,2:T(8,128)S(1)} %copy.22), channel_id=1, source_target_pairs={{0,1},{1,2},{2,3},{4,5},{5,6},{6,7},{8,9},{9,10},{10,11},{12,13},{... | collective-permute-start | bytes 42776 | tf_op jit(solution)/shard_map/ppermute | solution.py:18
  22.1 5.9 %collective-permute-start.5 = (f32[22,54,3]{1,0,2:T(8,128)S(1)}, f32[22,54,3]{1,0,2:T(8,128)S(1)}, u32[]{:S(2)}, u32[]{:S(2)}) collective-permute-start(f32[22,54,3]{1,0,2:T(8,128)S(1)} %copy.23), channel_id=1, source_target_pairs={{1,0},{2,1},{3,2},{5,4},{6,5},{7,6},{9,8},{10,9},{11,10},{13,12},{... | collective-permute-start | bytes 42776 | tf_op jit(solution)/shard_map/ppermute | solution.py:20
  40.1 0.7 copy-start.2
  40.1 0.7 copy-start.3
  42.8 3.0 %copy-start.8 = (pred[132]{0:T(512)(128)(4,1)S(1)}, pred[132]{0:T(512)(128)(4,1)}, u32[]{:S(2)}) copy-start(pred[132]{0:T(512)(128)(4,1)} %get-tuple-element.49) | copy-start | bytes 400
  42.8 3.0 %copy-start.9 = (pred[132]{0:T(512)(128)(4,1)S(1)}, pred[132]{0:T(512)(128)(4,1)}, u32[]{:S(2)}) copy-start(pred[132]{0:T(512)(128)(4,1)} %get-tuple-element.50) | copy-start | bytes 400
  46.5 4.2 %copy-start = (pred[18]{0:T(512)(128)(4,1)S(1)}, pred[18]{0:T(512)(128)(4,1)}, u32[]{:S(2)}) copy-start(pred[18]{0:T(512)(128)(4,1)} %get-tuple-element.51) | copy-start | bytes 58
  46.5 4.2 %copy-start.1 = (pred[18]{0:T(512)(128)(4,1)S(1)}, pred[18]{0:T(512)(128)(4,1)}, u32[]{:S(2)}) copy-start(pred[18]{0:T(512)(128)(4,1)} %get-tuple-element.52) | copy-start | bytes 58
  50.7 0.7 copy-start.6
  50.7 0.7 copy-start.7
  51.9 4.2 %copy-start.10 = (pred[130]{0:T(512)(128)(4,1)S(1)}, pred[130]{0:T(512)(128)(4,1)}, u32[]{:S(2)}) copy-start(pred[130]{0:T(512)(128)(4,1)} %get-tuple-element.55) | copy-start | bytes 394
  51.9 4.2 %copy-start.11 = (pred[130]{0:T(512)(128)(4,1)S(1)}, pred[130]{0:T(512)(128)(4,1)}, u32[]{:S(2)}) copy-start(pred[130]{0:T(512)(128)(4,1)} %get-tuple-element.56) | copy-start | bytes 394
where the time goes:
time: 102 us
  blocking collectives  40.2 us (39%)
  other arithmetic  24.7 us (24%)
  local copies, waits for them, and re-layouts  14.7 us (14%)
  starting transfers between devices  13.5 us (13%)
  waiting for transfers between devices  7.76 us (8%)
  between operations  1.03 us (1%)
    psum x1, blocking collectives, reduce_now(): return lax.psum(partial_value, ('gx', 'gy', 'gz'))  40.2 us
    ppermute x3, starting transfers between devices, extended_2(): lax.ppermute(tail, axis, [(i, (i + 1) % count) for i in range(ends)])  9.66 us
    ppermute x3, waiting for transfers between devices, extended_2(): lax.ppermute(head, axis, [((i + 1) % count, i) for i in range(ends)])  7.75 us
    sub x2, other arithmetic, update(): return center - pseudo_step * sgn * (jnp.sqrt(total) - 1.0)  6.34 us
    select_n x8, other arithmetic, clamp_axis(): jnp.where((place == count - 1) & (position >= length - margin), high_valu...  4.72 us
    ppermute x3, starting transfers between devices, extended_2(): lax.ppermute(head, axis, [((i + 1) % count, i) for i in range(ends)])  3.88 us
    reduce_sum x3, other arithmetic, local(): partials.append(reduce_now(jnp.sum(difference * difference)))  3.58 us
    broadcast_in_dim x6, local copies, waits for them, and re-layouts, clamp_axis(): jnp.where((place == count - 1) & (position >= length - margin), high_valu...  3.46 us
  transfers between devices with their start and end apart: 6, of which 3 were waited for; matrix products, arithmetic and copies ran while one was open for 4% of the time, Pallas kernels for 0%

commit v1 on v0

--- a/solution.py
+++ b/solution.py
@@ -2,6 +2,7 @@
 import jax.numpy as jnp
 from jax import lax
 from jax.sharding import PartitionSpec as P
+from jax.lax import psum
 
 ITERS = 3
 pseudo_step = 0.45
@@ -69,7 +70,13 @@
 
 
 def reduce_now(partial_value):
-    return lax.psum(partial_value, ("gx", "gy", "gz"))
+
+    def clusters_supply_all(s0, axis_key, device_axis):
+        for h in (axis_key, device_axis):
+            s0 = psum(s0, h)
+        return s0
+
+    return clusters_supply_all(partial_value, ("gy", "gz"), "gx")
 
 
 def local(phi_start):

time: 102 us -> 88.6 us (0.87)
  blocking collectives: 40.2 us -> 26.5 us
    psum x1 -> x2, blocking collectives: 40.2 us -> 26.5 us  [clusters_supply_all(): s0 = psum(s0, h)]
  transfers between devices with their start and end apart: 6 -> 6, of which waited for: 3 -> 3; matrix products, arithmetic and copies ran while one was open for 4% -> 5% of each run, Pallas kernels for 0% -> 0%
where the time goes in v1:
time: 88.6 us; the launch traced here: 88.1 us
  blocking collectives  26.5 us (30%)
  other arithmetic  24.6 us (28%)
  local copies, waits for them, and re-layouts  14.7 us (17%)
  starting transfers between devices  13.5 us (15%)
  waiting for transfers between devices  7.78 us (9%)
  between operations  1.03 us (1%)
    psum x2, blocking collectives, clusters_supply_all(): s0 = psum(s0, h)  26.5 us
    ppermute x3, starting transfers between devices, extended_2(): lax.ppermute(tail, axis, [(i, (i + 1) % count) for i in range(ends)])  9.66 us
    ppermute x3, waiting for transfers between devices, extended_2(): lax.ppermute(head, axis, [((i + 1) % count, i) for i in range(ends)])  7.77 us
    sub x2, other arithmetic, update(): return center - pseudo_step * sgn * (jnp.sqrt(total) - 1.0)  6.34 us
    select_n x8, other arithmetic, clamp_axis(): jnp.where((place == count - 1) & (position >= length - margin), high_valu...  4.72 us
    ppermute x3, starting transfers between devices, extended_2(): lax.ppermute(head, axis, [((i + 1) % count, i) for i in range(ends)])  3.88 us
    reduce_sum x3, other arithmetic, local(): partials.append(reduce_now(jnp.sum(difference * difference)))  3.62 us
    broadcast_in_dim x6, local copies, waits for them, and re-layouts, clamp_axis(): jnp.where((place == count - 1) & (position >= length - margin), high_valu...  3.46 us
  transfers between devices with their start and end apart: 6, of which 3 were waited for; matrix products, arithmetic and copies ran while one was open for 5% of the time, Pallas kernels for 0%

profile of v1, /device:TPU:0, one launch (start us, length us, event | category | flops | bytes accessed | tf_op | source)
XLA Modules:
  0.0 88.1 jit_solution(970028498442245687)
XLA Ops:
  0.6 1.1 %copy.19 = f32[16,48,128]{2,0,1:T(8,128)S(1)} copy(f32[16,48,128]{2,1,0:T(8,128)} %param.1) | data formatting | bytes 786432 | tf_op args[0]
  1.8 4.9 %collective-permute-start = (f32[3,48,128]{2,0,1:T(4,128)S(1)}, f32[3,48,128]{2,0,1:T(4,128)S(1)}, u32[]{:S(2)}, u32[]{:S(2)}) collective-permute-start(f32[3,48,128]{2,0,1:T(4,128)S(1)} %get-tuple-element.38), channel_id=1, source_target_pairs={{0,8},{8,16},{16,24},{1,9},{9,17},{17,25},{2,10},{10,18},{18,26},{... | collective-permute-start | bytes 221192 | tf_op jit(solution)/shard_map/ppermute | solution.py:19
  6.7 1.3 %collective-permute-start.1 = (f32[3,48,128]{2,0,1:T(4,128)S(1)}, f32[3,48,128]{2,0,1:T(4,128)S(1)}, u32[]{:S(2)}, u32[]{:S(2)}) collective-permute-start(f32[3,48,128]{2,0,1:T(4,128)S(1)} %get-tuple-element.39), channel_id=1, source_target_pairs={{8,0},{16,8},{24,16},{9,1},{17,9},{25,17},{10,2},{18,10},{26,18},{... | collective-permute-start | bytes 221192 | tf_op jit(solution)/shard_map/ppermute | solution.py:21
  8.0 0.0 copy-start.4
  8.1 0.0 copy-start.5
  8.1 0.6 compare_and_fusion.4
  8.6 0.5 compare_and_fusion.6
  9.1 0.6 compare_and_fusion.3
  9.7 0.5 compare_and_fusion.2
  10.3 0.0 collective-permute-done
  10.3 2.9 %collective-permute-done.1 = f32[3,48,128]{2,0,1:T(4,128)S(1)} collective-permute-done((f32[3,48,128]{2,0,1:T(4,128)S(1)}, f32[3,48,128]{2,0,1:T(4,128)S(1)}, u32[]{:S(2)}, u32[]{:S(2)}) %collective-permute-start.1) | collective-permute-done | bytes 73760 | tf_op jit(solution)/shard_map/ppermute | solution.py:21
  13.2 1.3 %collective-permute-start.2 = (f32[22,3,128]{2,0,1:T(8,128)S(1)}, f32[22,3,128]{2,0,1:T(8,128)S(1)}, u32[]{:S(2)}, u32[]{:S(2)}) collective-permute-start(f32[22,3,128]{2,0,1:T(8,128)S(1)} %get-tuple-element.36), channel_id=1, source_target_pairs={{0,4},{1,5},{2,6},{3,7},{8,12},{9,13},{10,14},{11,15},{16,20},{17,... | collective-permute-start | bytes 101384 | tf_op jit(solution)/shard_map/ppermute | solution.py:19
  14.5 1.3 %collective-permute-start.3 = (f32[22,3,128]{2,0,1:T(8,128)S(1)}, f32[22,3,128]{2,0,1:T(8,128)S(1)}, u32[]{:S(2)}, u32[]{:S(2)}) collective-permute-start(f32[22,3,128]{2,0,1:T(8,128)S(1)} %get-tuple-element.37), channel_id=1, source_target_pairs={{4,0},{5,1},{6,2},{7,3},{12,8},{13,9},{14,10},{15,11},{20,16},{21,... | collective-permute-start | bytes 101384 | tf_op jit(solution)/shard_map/ppermute | solution.py:21
  15.8 0.6 compare_and_fusion.1
  16.4 0.0 collective-permute-done.2
  16.4 1.2 %collective-permute-done.3 = f32[22,3,128]{2,0,1:T(8,128)S(1)} collective-permute-done((f32[22,3,128]{2,0,1:T(8,128)S(1)}, f32[22,3,128]{2,0,1:T(8,128)S(1)}, u32[]{:S(2)}, u32[]{:S(2)}) %collective-permute-start.3) | collective-permute-done | bytes 33824 | tf_op jit(solution)/shard_map/ppermute | solution.py:21
  17.6 0.1 pad_maximum_fusion.1
  17.7 0.2 fusion.12
  18.0 0.3 copy.22
  18.3 3.5 %collective-permute-start.4 = (f32[22,54,3]{1,0,2:T(8,128)S(1)}, f32[22,54,3]{1,0,2:T(8,128)S(1)}, u32[]{:S(2)}, u32[]{:S(2)}) collective-permute-start(f32[22,54,3]{1,0,2:T(8,128)S(1)} %copy.22), channel_id=1, source_target_pairs={{0,1},{1,2},{2,3},{4,5},{5,6},{6,7},{8,9},{9,10},{10,11},{12,13},{... | collective-permute-start | bytes 42776 | tf_op jit(solution)/shard_map/ppermute | solution.py:19
  21.8 0.3 copy.23
  22.1 1.3 %collective-permute-start.5 = (f32[22,54,3]{1,0,2:T(8,128)S(1)}, f32[22,54,3]{1,0,2:T(8,128)S(1)}, u32[]{:S(2)}, u32[]{:S(2)}) collective-permute-start(f32[22,54,3]{1,0,2:T(8,128)S(1)} %copy.23), channel_id=1, source_target_pairs={{1,0},{2,1},{3,2},{5,4},{6,5},{7,6},{9,8},{10,9},{11,10},{13,12},{... | collective-permute-start | bytes 42776 | tf_op jit(solution)/shard_map/ppermute | solution.py:21
  23.4 0.6 compare_and_fusion
  23.9 0.0 collective-permute-done.4
  23.9 0.4 copy.24
  24.3 3.6 %collective-permute-done.5 = f32[22,54,3]{1,0,2:T(8,128)S(1)} collective-permute-done((f32[22,54,3]{1,0,2:T(8,128)S(1)}, f32[22,54,3]{1,0,2:T(8,128)S(1)}, u32[]{:S(2)}, u32[]{:S(2)}) %collective-permute-start.5) | collective-permute-done | bytes 14288 | tf_op jit(solution)/shard_map/ppermute | solution.py:21
  27.9 0.4 copy.25
  28.3 0.8 pad_maximum_fusion
  29.1 0.1 fusion.7
  29.2 0.8 select_select_fusion.2
  30.1 0.0 copy-done.4
  30.1 1.0 %select_select_fusion.1 = f32[22,54,134]{2,0,1:T(8,128)S(1)} fusion(f32[22,134]{1,0:T(8,128)S(1)} %get-tuple-element.19, f32[22,134]{1,0:T(8,128)S(1)} %get-tuple-element.18, pred[54]{0:T(512)(128)(4,1)S(1)} %get-tuple-element.44, pred[54]{0:T(512)(128)(4,1)S(1)} %get-tuple-element.45, f32[54,134]{1,0:T(8,128)S(1)} %get-tuple-element.40, ...), kind=kLoop, calls=%fused_computation.3 | loop fusion | flops 1591920 | bytes 1355160 | tf_op jit(solution)/shard_map/jit(_where)/select_n | solution.py:57
  31.1 0.4 fusion.6
  31.6 0.4 copy.39
  32.0 0.4 copy.40
  32.4 3.3 %rsqrt_multiply_fusion = (f32[22,54,134]{2,0,1:T(8,128)S(1)}, f32[22,54,134]{2,0,1:T(8,128)S(1)}) fusion(f32[22,54]{0,1:T(8,128)S(1)} %bitcast.56, pred[134]{0:T(512)(128)(4,1)} %get-tuple-element.46, f32[22,54]{0,1:T(8,128)S(1)} %bitcast.55, pred[134]{0:T(512)(128)(4,1)} %get-tuple-element.47, f32[22,134]{1,0:T(8,128)S(1)} %get-tuple-element.19, ...), kind=kLoop, calls=%fused_computation.1 | loop fusion | flops 2387880 | bytes 2001700 | tf_op jit(solution)/shard_map/div | solution.py:29
  35.7 3.2 %multiply_subtract_fusion = f32[20,52,132]{2,0,1:T(8,128)S(1)} fusion(f32[22,54,134]{2,0,1:T(8,128)S(1)} %get-tuple-element.15, f32[22,54,134]{2,0,1:T(8,128)S(1)} %get-tuple-element.14), kind=kLoop, calls=%fused_computation.14 | loop fusion | flops 6314880 | bytes 4942080 | tf_op jit(solution)/shard_map/sub | solution.py:48
  39.0 1.0 %fusion.3 = f32[]{:T(128)} fusion(f32[22,54,134]{2,0,1:T(8,128)S(1)} %get-tuple-element.15, f32[20,52,132]{2,0,1:T(8,128)S(1)} %multiply_subtract_fusion), kind=kLoop, calls=%fused_computation.31 | loop fusion | flops 294911 | bytes 786436 | tf_op jit(solution)/shard_map/reduce_sum | solution.py:92
  40.0 0.1 fusion.9
  40.1 0.2 select_select_fusion.5
  40.4 0.3 copy-done.2
  40.7 0.0 copy-done.3
  40.7 0.5 select_select_fusion.4
  41.3 1.5 %fusion.8 = (f32[20,52,1]{2,0,1:T(8,128)}, f32[20,52,1]{2,0,1:T(8,128)}) fusion(f32[20,52,132]{2,0,1:T(8,128)S(1)} %select_select_fusion.4), kind=kLoop, calls=%fused_computation.78 | loop fusion | bytes 16640 | tf_op jit(solution)/shard_map/slice | solution.py:55
  42.7 1.5 %copy.42 = f32[20,52,1]{0,1,2:T(8,128)S(1)} copy(f32[20,52,1]{2,0,1:T(8,128)} %get-tuple-element.23) | data formatting | bytes 8320 | tf_op jit(solution)/shard_map/jit(_where)/broadcast_in_dim | solution.py:56
  44.3 1.5 %copy.41 = f32[20,52,1]{0,1,2:T(8,128)S(1)} copy(f32[20,52,1]{2,0,1:T(8,128)} %get-tuple-element.22) | data formatting | bytes 8320 | tf_op jit(solution)/shard_map/jit(_where)/broadcast_in_dim | solution.py:57
  45.8 0.0 copy-done.8
  45.8 0.6 select_select_fusion.3
  46.4 3.1 %multiply_subtract_fusion.1 = f32[18,50,130]{2,0,1:T(8,128)S(1)} fusion(f32[20,52,132]{2,0,1:T(8,128)S(1)} %select_select_fusion.3, f32[22,54,134]{2,0,1:T(8,128)S(1)} %get-tuple-element.14), kind=kLoop, calls=%fused_computation.24 | loop fusion | flops 5382000 | bytes 4212000 | tf_op jit(solution)/shard_map/sub | solution.py:48
  49.6 1.0 %fusion.1 = f32[]{:T(128)} fusion(f32[20,52,132]{2,0,1:T(8,128)S(1)} %select_select_fusion.3, f32[18,50,130]{2,0,1:T(8,128)S(1)} %multiply_subtract_fusion.1), kind=kLoop, calls=%fused_computation.28 | loop fusion | flops 294911 | bytes 786436 | tf_op jit(solution)/shard_map/reduce_sum | solution.py:92
  50.6 0.1 fusion.11
  50.7 0.2 select_select_fusion.8
  51.0 0.4 copy-done.6
  51.4 0.0 copy-done.7
  51.4 0.5 select_select_fusion.7
  51.9 1.2 %fusion.10 = (f32[18,50,1]{2,0,1:T(8,128)}, f32[18,50,1]{2,0,1:T(8,128)}) fusion(f32[18,50,130]{2,0,1:T(8,128)S(1)} %select_select_fusion.7), kind=kLoop, calls=%fused_computation.80 | loop fusion | bytes 14400 | tf_op jit(solution)/shard_map/slice | solution.py:55
  53.1 1.5 %copy.43 = f32[18,50,1]{0,1,2:T(8,128)S(1)} copy(f32[18,50,1]{2,0,1:T(8,128)} %get-tuple-element.28) | data formatting | bytes 7200 | tf_op jit(solution)/shard_map/jit(_where)/broadcast_in_dim | solution.py:57
  54.6 1.5 %copy.44 = f32[18,50,1]{0,1,2:T(8,128)S(1)} copy(f32[18,50,1]{2,0,1:T(8,128)} %get-tuple-element.29) | data formatting | bytes 7200 | tf_op jit(solution)/shard_map/jit(_where)/broadcast_in_dim | solution.py:56
  56.1 0.6 select_select_fusion.6
  56.8 1.6 %multiply_reduce_fusion = (f32[]{:T(128)}, f32[16,48,128]{2,0,1:T(8,128)S(1)}) fusion(f32[18,50,130]{2,0,1:T(8,128)S(1)} %select_select_fusion.6, f32[22,54,134]{2,0,1:T(8,128)S(1)} %get-tuple-element.14), kind=kLoop, calls=%fused_computation.38 | loop fusion | flops 4816895 | bytes 3538948 | tf_op jit(solution)/shard_map/reduce_sum | solution.py:92
  58.4 0.9 copy.38
  59.3 16.0 %all-reduce = (f32[]{:T(128)}, f32[]{:T(128)}, f32[]{:T(128)}) all-reduce(f32[]{:T(128)} %get-tuple-element.12, f32[]{:T(128)} %fusion.1, f32[]{:T(128)} %fusion.3), channel_id=1, replica_groups=mesh['gx'=4,'gy'=2,'gz'=4] {'gy','gz'}, use_global_device_ids=true, to_apply=%region_7.8 | all-reduce | flops 3 | bytes 24 | tf_op jit(solution)/shard_map/psum | solution.py:76
  75.2 10.5 %all-reduce.1 = (f32[1]{0:T(128)}, f32[1]{0:T(128)}, f32[1]{0:T(128)}) all-reduce(f32[1]{0:T(128)} %bitcast.20, f32[1]{0:T(128)} %bitcast.19, f32[1]{0:T(128)} %bitcast.18), channel_id=1, replica_groups=mesh['gx'=4,'gy'=2,'gz'=4] {'gx'}, use_global_device_ids=true, to_apply=%region_8.9 | all-reduce | flops 3 | bytes 24 | tf_op jit(solution)/shard_map/psum | solution.py:76
  85.7 2.4 %fusion.5 = f32[3]{0:T(128)} fusion(f32[1]{0:T(128)} %get-tuple-element.9, f32[1]{0:T(128)} %get-tuple-element.10, f32[1]{0:T(128)} %get-tuple-element.11), kind=kLoop, calls=%fused_computation.75 | loop fusion | flops 12 | bytes 24 | tf_op jit(solution)/shard_map/div | solution.py:99
  (29 shorter events, 0.2 us)
Async XLA Ops:
  1.8 8.5 %collective-permute-start = (f32[3,48,128]{2,0,1:T(4,128)S(1)}, f32[3,48,128]{2,0,1:T(4,128)S(1)}, u32[]{:S(2)}, u32[]{:S(2)}) collective-permute-start(f32[3,48,128]{2,0,1:T(4,128)S(1)} %get-tuple-element.38), channel_id=1, source_target_pairs={{0,8},{8,16},{16,24},{1,9},{9,17},{17,25},{2,10},{10,18},{18,26},{... | collective-permute-start | bytes 221192 | tf_op jit(solution)/shard_map/ppermute | solution.py:19
  6.7 6.5 %collective-permute-start.1 = (f32[3,48,128]{2,0,1:T(4,128)S(1)}, f32[3,48,128]{2,0,1:T(4,128)S(1)}, u32[]{:S(2)}, u32[]{:S(2)}) collective-permute-start(f32[3,48,128]{2,0,1:T(4,128)S(1)} %get-tuple-element.39), channel_id=1, source_target_pairs={{8,0},{16,8},{24,16},{9,1},{17,9},{25,17},{10,2},{18,10},{26,18},{... | collective-permute-start | bytes 221192 | tf_op jit(solution)/shard_map/ppermute | solution.py:21
  8.0 22.0 %copy-start.4 = (pred[54]{0:T(512)(128)(4,1)}, pred[54]{0:T(512)(128)(4,1)S(1)}, u32[]{:S(2)}) copy-start(pred[54]{0:T(512)(128)(4,1)S(1)} %get-tuple-element.44) | copy-start | bytes 166
  8.1 22.0 %copy-start.5 = (pred[54]{0:T(512)(128)(4,1)}, pred[54]{0:T(512)(128)(4,1)S(1)}, u32[]{:S(2)}) copy-start(pred[54]{0:T(512)(128)(4,1)S(1)} %get-tuple-element.45) | copy-start | bytes 166
  13.2 3.2 %collective-permute-start.2 = (f32[22,3,128]{2,0,1:T(8,128)S(1)}, f32[22,3,128]{2,0,1:T(8,128)S(1)}, u32[]{:S(2)}, u32[]{:S(2)}) collective-permute-start(f32[22,3,128]{2,0,1:T(8,128)S(1)} %get-tuple-element.36), channel_id=1, source_target_pairs={{0,4},{1,5},{2,6},{3,7},{8,12},{9,13},{10,14},{11,15},{16,20},{17,... | collective-permute-start | bytes 101384 | tf_op jit(solution)/shard_map/ppermute | solution.py:19
  14.5 3.1 %collective-permute-start.3 = (f32[22,3,128]{2,0,1:T(8,128)S(1)}, f32[22,3,128]{2,0,1:T(8,128)S(1)}, u32[]{:S(2)}, u32[]{:S(2)}) collective-permute-start(f32[22,3,128]{2,0,1:T(8,128)S(1)} %get-tuple-element.37), channel_id=1, source_target_pairs={{4,0},{5,1},{6,2},{7,3},{12,8},{13,9},{14,10},{15,11},{20,16},{21,... | collective-permute-start | bytes 101384 | tf_op jit(solution)/shard_map/ppermute | solution.py:21
  18.3 5.7 %collective-permute-start.4 = (f32[22,54,3]{1,0,2:T(8,128)S(1)}, f32[22,54,3]{1,0,2:T(8,128)S(1)}, u32[]{:S(2)}, u32[]{:S(2)}) collective-permute-start(f32[22,54,3]{1,0,2:T(8,128)S(1)} %copy.22), channel_id=1, source_target_pairs={{0,1},{1,2},{2,3},{4,5},{5,6},{6,7},{8,9},{9,10},{10,11},{12,13},{... | collective-permute-start | bytes 42776 | tf_op jit(solution)/shard_map/ppermute | solution.py:19
  22.1 5.9 %collective-permute-start.5 = (f32[22,54,3]{1,0,2:T(8,128)S(1)}, f32[22,54,3]{1,0,2:T(8,128)S(1)}, u32[]{:S(2)}, u32[]{:S(2)}) collective-permute-start(f32[22,54,3]{1,0,2:T(8,128)S(1)} %copy.23), channel_id=1, source_target_pairs={{1,0},{2,1},{3,2},{5,4},{6,5},{7,6},{9,8},{10,9},{11,10},{13,12},{... | collective-permute-start | bytes 42776 | tf_op jit(solution)/shard_map/ppermute | solution.py:21
  40.1 0.6 copy-start.2
  40.1 0.6 copy-start.3
  42.7 3.0 %copy-start.8 = (pred[132]{0:T(512)(128)(4,1)S(1)}, pred[132]{0:T(512)(128)(4,1)}, u32[]{:S(2)}) copy-start(pred[132]{0:T(512)(128)(4,1)} %get-tuple-element.52) | copy-start | bytes 400
  42.7 3.0 %copy-start.9 = (pred[132]{0:T(512)(128)(4,1)S(1)}, pred[132]{0:T(512)(128)(4,1)}, u32[]{:S(2)}) copy-start(pred[132]{0:T(512)(128)(4,1)} %get-tuple-element.53) | copy-start | bytes 400
  46.4 4.3 %copy-start = (pred[18]{0:T(512)(128)(4,1)S(1)}, pred[18]{0:T(512)(128)(4,1)}, u32[]{:S(2)}) copy-start(pred[18]{0:T(512)(128)(4,1)} %get-tuple-element.54) | copy-start | bytes 58
  46.4 4.3 %copy-start.1 = (pred[18]{0:T(512)(128)(4,1)S(1)}, pred[18]{0:T(512)(128)(4,1)}, u32[]{:S(2)}) copy-start(pred[18]{0:T(512)(128)(4,1)} %get-tuple-element.55) | copy-start | bytes 58
  50.7 0.7 copy-start.6
  50.7 0.7 copy-start.7
  51.9 4.2 %copy-start.10 = (pred[130]{0:T(512)(128)(4,1)S(1)}, pred[130]{0:T(512)(128)(4,1)}, u32[]{:S(2)}) copy-start(pred[130]{0:T(512)(128)(4,1)} %get-tuple-element.58) | copy-start | bytes 394
  51.9 4.2 %copy-start.11 = (pred[130]{0:T(512)(128)(4,1)S(1)}, pred[130]{0:T(512)(128)(4,1)}, u32[]{:S(2)}) copy-start(pred[130]{0:T(512)(128)(4,1)} %get-tuple-element.59) | copy-start | bytes 394
